TPU v7x, 32 devices: a whole 2x2x4 slice. The times are simulated.
32 devices in a mesh: gy: 8 (over z, x), gx: 4 (over y, core).
Axes of the slice: x: 2, y: 2, z: 4, core: 2. Of those that a mesh axis runs over, the one named last changes fastest.
Arguments:
- tall_factor: bfloat16 [8192, 2048], P('gy', 'gx'), may hold values from -6 to 6
- wide_factor: bfloat16 [2048, 4096], P('gy', 'gx'), may hold values from -0.125 to 0.125
- target: float32 [8192, 4096], P('gy', 'gx'), may hold values from -6 to 6
Outputs:
- product_sum: float32 [8192, 4096], P('gy', 'gx')
All inputs are finite; a program needn't handle non-finite values.
Results may differ from a plain program's by a relative error of at most 0.0003.
Values may be sent and summed in bfloat16 or wider, within the bound.
A program may use at most 128 MiB of HBM per device.

v0:
```python
import jax
import jax.numpy as jnp
from jax import lax
from jax.sharding import PartitionSpec as P


def taken_in(section, axis, dim, lap, start):
    def gathered(part):
        return lax.all_gather(part, axis, axis=dim, tiled=True)

    return lap(start, jax.tree.map(gathered, section), jnp.int32(0))


def join_panel(carry, left_panel, right_panel):
    return carry + jnp.dot(left_panel, right_panel, preferred_element_type=jnp.float32)


def on_device(tall_factor, wide_factor, target):
    begin = jnp.zeros((tall_factor.shape[0], wide_factor.shape[1]), jnp.float32)
    left_line = lax.all_gather(tall_factor, "gx", axis=1, tiled=True)

    def take_rows(carry, piece, start):
        left_piece = lax.dynamic_slice_in_dim(left_line, start, piece.shape[0], axis=1)
        return join_panel(carry, left_piece, piece)

    total = taken_in(wide_factor, "gy", 0, take_rows, begin)
    product_sum = target - total
    row_power = lax.psum(jnp.sum(product_sum * product_sum, axis=1), "gx")
    product_sum = (
        product_sum
        * lax.rsqrt(row_power / (product_sum.shape[1] * lax.axis_size("gx")) + 1e-06)[:, None]
    )
    return product_sum


def solution(mesh):
    return jax.shard_map(
        on_device,
        mesh=mesh,
        in_specs=(P("gy", "gx"), P("gy", "gx"), P("gy", "gx")),
        out_specs=P("gy", "gx"),
        check_vma=False,
    )
```

profile of v0, /device:TPU:0, one launch (start us, length us, event | category | flops | bytes accessed | tf_op | source)
XLA Modules:
  0.0 155.4 jit_solution(12691582396637993418)
XLA Ops:
  6.5 0.0 all-gather.3.cloned.1.call-start
  6.5 0.7 all-gather.3.cloned.1.call-update
  7.3 0.0 all-gather.5.cloned.1.call-start
  7.3 0.7 all-gather.5.cloned.1.call-update
  8.0 5.3 %copy.4 = f32[1024,1024]{0,1:T(8,128)} copy(f32[1024,1024]{1,0:T(8,128)} %param.5) | data formatting | bytes 8388608 | tf_op args[2]
  13.4 32.7 %all-gather.3.cloned.1.call-done = bf16[1024,2048]{1,0:T(8,128)(2,1)} async-done(((bf16[1024,512]{1,0:T(8,128)(2,1)}), bf16[1024,2048]{1,0:T(8,128)(2,1)}) %all-gather.3.cloned.1.call-update) | async-done | bytes 4194320 | tf_op jit(solution)/shard_map/all_gather | solution.py:20
  46.0 75.3 %all-gather.5.cloned.1.call-done = bf16[2048,1024]{1,0:T(8,128)(2,1)} async-done(((bf16[256,1024]{1,0:T(8,128)(2,1)}), bf16[2048,1024]{1,0:T(8,128)(2,1)}) %all-gather.5.cloned.1.call-update) | async-done | bytes 4194320 | tf_op jit(solution)/shard_map/all_gather | solution.py:9
  121.3 11.3 %multiply_reduce_fusion = (f32[1024]{0:T(1024)S(1)}, f32[1024,1024]{0,1:T(8,128)}) fusion(f32[1024,1024]{0,1:T(8,128)} %copy.4, bf16[1024,2048]{1,0:T(8,128)(2,1)} %all-gather.3.cloned.1.call-done, bf16[2048,1024]{1,0:T(8,128)(2,1)} %all-gather.5.cloned.1.call-done), kind=kOutput, calls=%fused_computation | convolution fusion | flops 4298112000 | bytes 16781312 | tf_op jit(solution)/shard_map/dot_general | solution.py:15
  132.6 5.6 %psum.7 = f32[1024]{0:T(1024)S(1)} all-reduce(f32[1024]{0:T(1024)S(1)} %get-tuple-element.5), channel_id=1, replica_groups=mesh['gy'=8,'gx'=4] {'gx'}, use_global_device_ids=true, to_apply=%region_1.0 | all-reduce | flops 1024 | bytes 8192 | tf_op jit(solution)/shard_map/psum | solution.py:28
  138.3 5.0 %broadcast_multiply_fusion = f32[1024,1024]{0,1:T(8,128)} fusion(f32[1024,1024]{0,1:T(8,128)} %get-tuple-element.6, f32[1024]{0:T(1024)S(1)} %add_rsqrt_fusion), kind=kLoop, calls=%fused_computation.1 | loop fusion | flops 1048576 | bytes 8392704 | tf_op jit(solution)/shard_map/mul | solution.py:30
  143.2 5.3 %copy.5 = f32[1024,1024]{1,0:T(8,128)} copy(f32[1024,1024]{0,1:T(8,128)} %broadcast_multiply_fusion) | data formatting | bytes 8388608 | tf_op jit(solution)/shard_map/mul | solution.py:30
  (1 shorter events, 0.0 us)
Async XLA Ops:
  6.5 39.5 %all-gather.3.cloned.1.call-start = ((), (), s32[]{:S(2)}) async-start(), calls=%async_computation | async-start | bytes 5242880 | tf_op jit(solution)/shard_map/all_gather | solution.py:20
  7.3 114.0 %all-gather.5.cloned.1.call-start = ((), (), s32[]{:S(2)}) async-start(), calls=%async_computation.1 | async-start | bytes 4718592 | tf_op jit(solution)/shard_map/all_gather | solution.py:9
Sparse Core Ops, SparseCore 0:
  8.9 37.0 all-gather.2
  48.2 73.0 all-gather.4
where the time goes:
time: 156 us; the launch traced here: 155 us
  waiting for transfers between devices  109 us (70%)
  between operations  13.4 us (9%)
  matrix products  11.3 us (7%)
  local copies, waits for them, and re-layouts  10.7 us (7%)
  blocking collectives  5.63 us (4%)
  other arithmetic  4.99 us (3%)
    all_gather x1, waiting for transfers between devices, gathered(): return lax.all_gather(part, axis, axis=dim, tiled=True)  75.3 us
    all_gather x1, waiting for transfers between devices, on_device(): left_line = lax.all_gather(tall_factor, 'gx', axis=1, tiled=True)  32.7 us
    dot_general x1, matrix products, join_panel(): jnp.dot(left_panel, right_panel, preferred_element_type=jnp.float32)  11.3 us
    psum x1, blocking collectives, on_device(): row_power = lax.psum(jnp.sum(product_sum * product_sum, axis=1), 'gx')  5.63 us
    unnamed x1, local copies, waits for them, and re-layouts  5.35 us
    mul x1, local copies, waits for them, and re-layouts, on_device(): product_sum * lax.rsqrt(row_power / (product_sum.shape[1] * lax.axis_size...  5.34 us
    mul x1, other arithmetic, on_device(): product_sum * lax.rsqrt(row_power / (product_sum.shape[1] * lax.axis_size...  4.98 us
  transfers between devices with their start and end apart: 2, of which 2 were waited for; matrix products, arithmetic and copies ran while one was open for 3% of the time, Pallas kernels for 0%

commit v1 on v0

v1 whole, which is shorter than its diff:
```python
import functools

import jax
import jax.numpy as jnp
from jax import lax
from jax.experimental import pallas as pl
from jax.experimental.pallas import tpu as pltpu
from jax.sharding import PartitionSpec as P

MESH = pl.DeviceIdType.MESH
LANES = 128
HALVES = 2


def kernel(
    n, m, a_hbm, b_hbm, t_hbm, o_hbm, p_out,
    a_buf, b_buf, acc, p_buf,
    a_recv, b_recv, p_recv, a_send, b_send, p_send, l_sem,
):
    gy, gx = lax.axis_index("gy"), lax.axis_index("gx")
    depth, cols = b_hbm.shape
    rows = a_hbm.shape[0]
    per = a_hbm.shape[1] // depth
    wide = cols // HALVES
    line = n // 2
    z, x = gy // 2, gy % 2
    has_left, has_right = z > 0, z < line - 1
    left, right, across = gy - 2, gy + 2, z * 2 + 1 - x
    mate = (gx // 2) * 2 + 1 - gx % 2
    others = [lax.rem(gx + j, m) for j in range(1, m)]
    far = [lax.rem(gx + 2 * j, m) for j in range(1, m // 2)]

    loads_b = pltpu.make_async_copy(b_hbm, b_buf.at[gy], l_sem.at[0])
    loads_b.start()
    loads_a = []
    for i in range(per):
        c = pltpu.make_async_copy(
            a_hbm.at[:, pl.ds(i * depth, depth)], a_buf.at[gx * per + i], l_sem.at[2 + i]
        )
        c.start()
        loads_a.append(c)
    load_t = pltpu.make_async_copy(t_hbm, acc, l_sem.at[1])
    load_t.start()

    barrier = pltpu.get_barrier_semaphore()
    for g in others:
        pl.semaphore_signal(barrier, 1, device_id=(gy, g), device_id_type=MESH)
    pl.semaphore_signal(barrier, 1, device_id=(across, gx), device_id_type=MESH)

    @pl.when(has_left)
    def _():
        pl.semaphore_signal(barrier, 1, device_id=(left, gx), device_id_type=MESH)

    @pl.when(has_right)
    def _():
        pl.semaphore_signal(barrier, 1, device_id=(right, gx), device_id_type=MESH)

    pl.semaphore_wait(
        barrier, m + has_left.astype(jnp.int32) + has_right.astype(jnp.int32)
    )

    sends = []

    def when(cond, f):
        if cond is None:
            f()
        else:
            pl.when(cond)(f)

    def both(p, q):
        return q if p is None else jnp.logical_and(p, q)

    def b_copy(way, to, k, h):
        part = b_buf.at[k, :, pl.ds(h * wide, wide)]
        return pltpu.make_async_remote_copy(
            part, part, b_send.at[way, k, h], b_recv.at[k, h],
            device_id=(to, gx), device_id_type=MESH,
        )

    def send_b(cond, way, to, k, h):
        make = functools.partial(b_copy, way, to, k, h)
        when(cond, lambda: make().start())
        sends.append((cond, make))

    def a_copy(way, to, k):
        return pltpu.make_async_remote_copy(
            a_buf.at[k], a_buf.at[k], a_send.at[way, k], a_recv.at[k],
            device_id=(gy, to), device_id_type=MESH,
        )

    def send_a(way, to, k):
        make = functools.partial(a_copy, way, to, k)
        make().start()
        sends.append((None, make))

    def wait_b(k, h):
        b_copy(0, gy, k, h).wait_recv()

    def wait_a(k):
        a_copy(0, gx, k).wait_recv()

    tile = min(rows, 512)

    def multiply(k, h):
        at = pl.multiple_of(h * wide, wide)

        @pl.loop(0, rows // tile)
        def _(i):
            r = pl.ds(pl.multiple_of(i * tile, tile), tile)
            acc[r, pl.ds(at, wide)] -= jnp.dot(
                a_buf[k, r, :], b_buf[k, :, pl.ds(at, wide)],
                preferred_element_type=jnp.float32,
            )

    loads_b.wait()
    for h in range(HALVES):
        send_b(has_right, 0, right, gy, h)
        send_b(has_left, 1, left, gy, h)
        send_b(None, 2, across, gy, h)
    for i in range(per):
        loads_a[i].wait()
        for j, g in enumerate(far):
            send_a(1 + j, g, gx * per + i)
    for i in range(per):
        send_a(0, mate, gx * per + i)

    def side(d):
        return ((z - d, z - d >= 0), (z + d, z + d < line))

    def take_line(d, h):
        for way, (s, there) in enumerate(side(d)):
            k = s * 2 + x
            when(there, functools.partial(wait_b, k, h))
            onward, to = (has_right, right) if way == 0 else (has_left, left)
            send_b(both(there, onward), way, to, k, h)
            if d > 1 or h == 1:
                send_b(there, 2, across, k, h)

    def take_left(i):
        for g in far:
            wait_a(g * per + i)
            send_a(0, mate, g * per + i)

    def multiply_line(d):
        @pl.loop(0, 2 * HALVES)
        def _(e):
            w, h = e // HALVES, e % HALVES
            s = z + (2 * w - 1) * d

            @pl.when(jnp.logical_and(s >= 0, s < line))
            def _():
                multiply(s * 2 + x, h)

    def wait_multiply_across(d, h_list):
        for h in h_list:
            @pl.loop(0, 2)
            def _(w):
                s = z + (2 * w - 1) * d

                @pl.when(jnp.logical_and(s >= 0, s < line))
                def _():
                    k = s * 2 + 1 - x
                    wait_b(k, h)
                    multiply(k, h)

    middle = line // 2
    taken_left = 0
    for d in range(1, line):
        for h in range(HALVES):
            take_line(d, h)
        upto = min(per, (per * d + middle - 1) // middle)
        for i in range(taken_left, upto):
            take_left(i)
        taken_left = max(taken_left, upto)
        if d == middle:
            for i in range(taken_left, per):
                take_left(i)
            taken_left = per
            for i in range(per):
                wait_a(mate * per + i)
                for g in far:
                    wait_a((g // 2 * 2 + 1 - g % 2) * per + i)
            load_t.wait()

            @pl.loop(0, HALVES)
            def _(h):
                multiply(gy, h)

            for h in range(HALVES):
                wait_b(across, h)

            @pl.loop(0, HALVES)
            def _(h):
                multiply(across, h)

            for e in range(1, d):
                multiply_line(e)
    send_b(has_right, 0, right, across, 0)
    send_b(has_left, 1, left, across, 0)
    for d in range(middle, line):
        multiply_line(d)
    wait_multiply_across(1, [1])
    for d in range(2, line - 1):
        wait_multiply_across(d, [0, 1])
    wait_multiply_across(1, [0])
    if line - 1 > 1:
        wait_multiply_across(line - 1, [0, 1])

    store = pltpu.make_async_copy(acc, o_hbm, l_sem.at[0])
    store.start()

    @pl.loop(0, rows // LANES)
    def _(i):
        r = pl.ds(pl.multiple_of(i * LANES, LANES), LANES)
        part = jnp.zeros((LANES, LANES), jnp.float32)
        for c in range(cols // LANES):
            v = acc[r, pl.ds(c * LANES, LANES)]
            part += v * v
        p_buf[gx, pl.ds(i, 1), :] = jnp.sum(part.T, axis=0, keepdims=True)

    def p_copy(j, g, slot):
        return pltpu.make_async_remote_copy(
            p_buf.at[slot], p_buf.at[slot], p_send.at[j], p_recv.at[slot],
            device_id=(gy, g), device_id_type=MESH,
        )

    for j, g in enumerate(others):
        p_copy(j, g, gx).start()
    for cond, make in sends:
        when(cond, lambda make=make: make().wait_send())
    for j, g in enumerate(others):
        p_copy(j, g, g).wait_recv()
    total = p_buf[0]
    for g in range(1, m):
        total = total + p_buf[g]
    p_out[...] = total
    for j, g in enumerate(others):
        p_copy(j, g, gx).wait_send()
    store.wait()


def solution(mesh):
    n, m = mesh.shape["gy"], mesh.shape["gx"]

    def on_device(tall_factor, wide_factor, target):
        rows, (depth, cols) = tall_factor.shape[0], wide_factor.shape
        per = tall_factor.shape[1] // depth
        product_sum, row_power = pl.pallas_call(
            functools.partial(kernel, n, m),
            out_shape=(
                jax.ShapeDtypeStruct((rows, cols), jnp.float32),
                jax.ShapeDtypeStruct((rows // LANES, LANES), jnp.float32),
            ),
            in_specs=[pl.BlockSpec(memory_space=pl.ANY)] * 3,
            out_specs=(
                pl.BlockSpec(memory_space=pl.ANY),
                pl.BlockSpec(memory_space=pltpu.VMEM),
            ),
            scratch_shapes=[
                pltpu.VMEM((n, rows, depth), tall_factor.dtype),
                pltpu.VMEM((n, depth, cols), wide_factor.dtype),
                pltpu.VMEM((rows, cols), jnp.float32),
                pltpu.VMEM((m, rows // LANES, LANES), jnp.float32),
                pltpu.SemaphoreType.DMA((n,)),
                pltpu.SemaphoreType.DMA((n, HALVES)),
                pltpu.SemaphoreType.DMA((m,)),
                pltpu.SemaphoreType.DMA((max(2, m // 2), n)),
                pltpu.SemaphoreType.DMA((3, n, HALVES)),
                pltpu.SemaphoreType.DMA((m,)),
                pltpu.SemaphoreType.DMA((2 + per,)),
            ],
            compiler_params=pltpu.CompilerParams(
                collective_id=0, has_side_effects=True, vmem_limit_bytes=56 * 2**20
            ),
        )(tall_factor, wide_factor, target)
        scale = lax.rsqrt(row_power.reshape(rows) / (cols * m) + 1e-06)
        return product_sum * scale[:, None]

    return jax.shard_map(
        on_device,
        mesh=mesh,
        in_specs=(P("gy", "gx"), P("gy", "gx"), P("gy", "gx")),
        out_specs=P("gy", "gx"),
        check_vma=False,
    )
```

time: 156 us -> 59.4 us (0.38)
  waiting for transfers between devices: 109 us -> 0 us
  Pallas kernels: 0 us -> 54 us
  between operations: 13.4 us -> 0.01 us
  matrix products: 11.3 us -> 0 us
  local copies, waits for them, and re-layouts: 10.7 us -> 0 us
  blocking collectives: 5.63 us -> 0 us
    all_gather x2 -> x0, waiting for transfers between devices: 108 us -> none  [the longest x1 75.3 us: gathered(): return lax.all_gather(part, axis, axis=dim, tiled=True)]
    pallas_call x0 -> x1, Pallas kernels: none -> 54 us  [on_device(): pl.pallas_call(functools.partial(kernel, n, m), out_shape=(jax.ShapeDtype...]
    dot_general x1 -> x0, matrix products: 11.3 us -> none  [join_panel(): jnp.dot(left_panel, right_panel, preferred_element_type=jnp.float32)]
    psum x1 -> x0, blocking collectives: 5.63 us -> none  [on_device(): row_power = lax.psum(jnp.sum(product_sum * product_sum, axis=1), 'gx')]
    unnamed x1 -> x0, local copies, waits for them, and re-layouts: 5.35 us -> none
    mul x1 -> x0, local copies, waits for them, and re-layouts: 5.34 us -> none  [on_device(): product_sum * lax.rsqrt(row_power / (product_sum.shape[1] * lax.axis_size...]
  transfers between devices with their start and end apart: 2 -> 0, of which waited for: 2 -> 0; matrix products, arithmetic and copies ran while one was open for 3% -> 0% of each run, Pallas kernels for 0% -> 0%
where the time goes in v1:
time: 59.4 us; the launch traced here: 59.2 us
  Pallas kernels  54 us (91%)
  other arithmetic  5.22 us (9%)
    pallas_call x1, Pallas kernels, on_device(): pl.pallas_call(functools.partial(kernel, n, m), out_shape=(jax.ShapeDtype...  54 us
    mul x1, other arithmetic, on_device(): return product_sum * scale[:, None]  4.54 us

profile of v1, /device:TPU:0, one launch (start us, length us, event | category | flops | bytes accessed | tf_op | source)
XLA Modules:
  0.0 59.2 jit_solution(5077809340357365092)
XLA Ops:
  0.0 54.0 %shard_map.37 = (f32[1024,1024]{1,0:T(8,128)}, f32[8,128]{1,0:T(8,128)}) custom-call(bf16[1024,512]{1,0:T(8,128)(2,1)} %a_hbm.1, bf16[256,1024]{1,0:T(8,128)(2,1)} %b_hbm.1, f32[1024,1024]{1,0:T(8,128)} %t_hbm.1), custom_call_target="tpu_custom_call" | custom-call | tf_op jit(solution)/shard_map/pallas_call | solution.py:248
  54.0 0.7 %rsqrt_bitcast_fusion = f32[1024]{0:T(1024)S(1)} fusion(f32[8,128]{1,0:T(8,128)} %get-tuple-element.8), kind=kLoop, calls=%fused_computation.1 | loop fusion | flops 2048 | bytes 8192 | tf_op jit(solution)/shard_map/rsqrt | solution.py:276
  54.7 4.5 %broadcast_multiply_fusion = f32[1024,1024]{1,0:T(8,128)} fusion(f32[1024,1024]{1,0:T(8,128)} %get-tuple-element.7, f32[1024]{0:T(1024)S(1)} %rsqrt_bitcast_fusion), kind=kLoop, calls=%fused_computation | loop fusion | flops 1048576 | bytes 8392704 | tf_op jit(solution)/shard_map/mul | solution.py:277

commit v2 on v1

--- a/solution.py
+++ b/solution.py
@@ -9,19 +9,19 @@
 
 MESH = pl.DeviceIdType.MESH
 LANES = 128
-HALVES = 2
+PARTS = 4
 
 
 def kernel(
-    n, m, a_hbm, b_hbm, t_hbm, o_hbm, p_out,
-    a_buf, b_buf, acc, p_buf,
+    n, m, a_hbm, b_hbm, t_hbm, acc, p_out,
+    a_buf, b_buf, p_buf,
     a_recv, b_recv, p_recv, a_send, b_send, p_send, l_sem,
 ):
     gy, gx = lax.axis_index("gy"), lax.axis_index("gx")
     depth, cols = b_hbm.shape
     rows = a_hbm.shape[0]
     per = a_hbm.shape[1] // depth
-    wide = cols // HALVES
+    wide = cols // PARTS
     line = n // 2
     z, x = gy // 2, gy % 2
     has_left, has_right = z > 0, z < line - 1
@@ -113,7 +113,7 @@
             )
 
     loads_b.wait()
-    for h in range(HALVES):
+    for h in range(PARTS):
         send_b(has_right, 0, right, gy, h)
         send_b(has_left, 1, left, gy, h)
         send_b(None, 2, across, gy, h)
@@ -133,7 +133,7 @@
             when(there, functools.partial(wait_b, k, h))
             onward, to = (has_right, right) if way == 0 else (has_left, left)
             send_b(both(there, onward), way, to, k, h)
-            if d > 1 or h == 1:
+            if d > 1 or h < PARTS // 2:
                 send_b(there, 2, across, k, h)
 
     def take_left(i):
@@ -141,10 +141,9 @@
             wait_a(g * per + i)
             send_a(0, mate, g * per + i)
 
-    def multiply_line(d):
-        @pl.loop(0, 2 * HALVES)
-        def _(e):
-            w, h = e // HALVES, e % HALVES
+    def multiply_line(d, h):
+        @pl.loop(0, 2)
+        def _(w):
             s = z + (2 * w - 1) * d
 
             @pl.when(jnp.logical_and(s >= 0, s < line))
@@ -166,8 +165,12 @@
     middle = line // 2
     taken_left = 0
     for d in range(1, line):
-        for h in range(HALVES):
+        for h in range(PARTS):
             take_line(d, h)
+            if d > middle:
+                multiply_line(d - 1, h)
+                if d == middle + 1 and h < PARTS // 2:
+                    wait_multiply_across(1, [h])
         upto = min(per, (per * d + middle - 1) // middle)
         for i in range(taken_left, upto):
             take_left(i)
@@ -182,32 +185,38 @@
                     wait_a((g // 2 * 2 + 1 - g % 2) * per + i)
             load_t.wait()
 
-            @pl.loop(0, HALVES)
+            @pl.loop(0, PARTS)
             def _(h):
                 multiply(gy, h)
 
-            for h in range(HALVES):
+            for h in range(PARTS):
                 wait_b(across, h)
 
-            @pl.loop(0, HALVES)
+            @pl.loop(0, PARTS)
             def _(h):
                 multiply(across, h)
 
             for e in range(1, d):
-                multiply_line(e)
-    send_b(has_right, 0, right, across, 0)
-    send_b(has_left, 1, left, across, 0)
-    for d in range(middle, line):
-        multiply_line(d)
-    wait_multiply_across(1, [1])
+                @pl.loop(0, PARTS)
+                def _(h):
+                    multiply_line(e, h)
+
+    for h in range(PARTS // 2, PARTS):
+        send_b(has_right, 0, right, across, h)
+        send_b(has_left, 1, left, across, h)
+
+    @pl.loop(0, PARTS)
+    def _(h):
+        multiply_line(line - 1, h)
+
+    early, late = list(range(PARTS // 2)), list(range(PARTS // 2, PARTS))
+    if line <= middle + 1:
+        wait_multiply_across(1, early)
     for d in range(2, line - 1):
-        wait_multiply_across(d, [0, 1])
-    wait_multiply_across(1, [0])
+        wait_multiply_across(d, early + late)
+    wait_multiply_across(1, late)
     if line - 1 > 1:
-        wait_multiply_across(line - 1, [0, 1])
-
-    store = pltpu.make_async_copy(acc, o_hbm, l_sem.at[0])
-    store.start()
+        wait_multiply_across(line - 1, early + late)
 
     @pl.loop(0, rows // LANES)
     def _(i):
@@ -236,7 +245,6 @@
     p_out[...] = total
     for j, g in enumerate(others):
         p_copy(j, g, gx).wait_send()
-    store.wait()
 
 
 def solution(mesh):
@@ -248,29 +256,28 @@
         product_sum, row_power = pl.pallas_call(
             functools.partial(kernel, n, m),
             out_shape=(
-                jax.ShapeDtypeStruct((rows, cols), jnp.float32),
+                pltpu.VMEM((rows, cols), jnp.float32),
                 jax.ShapeDtypeStruct((rows // LANES, LANES), jnp.float32),
             ),
-            in_specs=[pl.BlockSpec(memory_space=pl.ANY)] * 3,
+            in_specs=[pl.BlockSpec(memory_space=pltpu.HBM)] * 3,
             out_specs=(
-                pl.BlockSpec(memory_space=pl.ANY),
+                pl.BlockSpec(memory_space=pltpu.VMEM),
                 pl.BlockSpec(memory_space=pltpu.VMEM),
             ),
             scratch_shapes=[
                 pltpu.VMEM((n, rows, depth), tall_factor.dtype),
                 pltpu.VMEM((n, depth, cols), wide_factor.dtype),
-                pltpu.VMEM((rows, cols), jnp.float32),
                 pltpu.VMEM((m, rows // LANES, LANES), jnp.float32),
                 pltpu.SemaphoreType.DMA((n,)),
-                pltpu.SemaphoreType.DMA((n, HALVES)),
+                pltpu.SemaphoreType.DMA((n, PARTS)),
                 pltpu.SemaphoreType.DMA((m,)),
                 pltpu.SemaphoreType.DMA((max(2, m // 2), n)),
-                pltpu.SemaphoreType.DMA((3, n, HALVES)),
+                pltpu.SemaphoreType.DMA((3, n, PARTS)),
                 pltpu.SemaphoreType.DMA((m,)),
                 pltpu.SemaphoreType.DMA((2 + per,)),
             ],
             compiler_params=pltpu.CompilerParams(
-                collective_id=0, has_side_effects=True, vmem_limit_bytes=56 * 2**20
+                collective_id=0, has_side_effects=True, vmem_limit_bytes=67043328 - rows * cols * 4 - 2**17
             ),
         )(tall_factor, wide_factor, target)
         scale = lax.rsqrt(row_power.reshape(rows) / (cols * m) + 1e-06)

time: 59.4 us -> 59.2 us (level)
  other arithmetic: 5.22 us -> 3.04 us
  Pallas kernels: 54 us -> 56 us
    mul x1, other arithmetic: 4.54 us -> 2.36 us  [on_device(): return product_sum * scale[:, None]]
    pallas_call x1, Pallas kernels: 54 us -> 56 us  [on_device(): pl.pallas_call(functools.partial(kernel, n, m), out_shape=(pltpu.VMEM((ro...]
where the time goes in v2:
time: 59.2 us; the launch traced here: 59 us
  Pallas kernels  56 us (95%)
  other arithmetic  3.04 us (5%)
    pallas_call x1, Pallas kernels, on_device(): pl.pallas_call(functools.partial(kernel, n, m), out_shape=(pltpu.VMEM((ro...  56 us
    mul x1, other arithmetic, on_device(): return product_sum * scale[:, None]  2.36 us

profile of v2, /device:TPU:0, one launch (start us, length us, event | category | flops | bytes accessed | tf_op | source)
XLA Modules:
  0.0 59.0 jit_solution(5512179406698321246)
XLA Ops:
  0.0 56.0 %shard_map.37 = (f32[1024,1024]{1,0:T(8,128)S(1)}, f32[8,128]{1,0:T(8,128)}) custom-call(bf16[1024,512]{1,0:T(8,128)(2,1)} %a_hbm.1, bf16[256,1024]{1,0:T(8,128)(2,1)} %b_hbm.1, f32[1024,1024]{1,0:T(8,128)} %t_hbm.1), custom_call_target="tpu_custom_call" | custom-call | tf_op jit(solution)/shard_map/pallas_call | solution.py:256
  56.0 0.7 %rsqrt_bitcast_fusion = f32[1024]{0:T(1024)S(1)} fusion(f32[8,128]{1,0:T(8,128)} %get-tuple-element.8), kind=kLoop, calls=%fused_computation.1 | loop fusion | flops 2048 | bytes 8192 | tf_op jit(solution)/shard_map/rsqrt | solution.py:283
  56.7 2.4 %broadcast_multiply_fusion = f32[1024,1024]{1,0:T(8,128)} fusion(f32[1024,1024]{1,0:T(8,128)S(1)} %get-tuple-element.7, f32[1024]{0:T(1024)S(1)} %rsqrt_bitcast_fusion), kind=kLoop, calls=%fused_computation | loop fusion | flops 1048576 | bytes 8392704 | tf_op jit(solution)/shard_map/mul | solution.py:284
